TPU v7x, 32 devices: a whole 2x2x4 slice. The times are simulated.
32 devices in a mesh: rows: 4 (over y, core), cols: 8 (over z, x).
Axes of the slice: x: 2, y: 2, z: 4, core: 2. Of those that a mesh axis runs over, the one named last changes fastest.
Arguments:
- left_factors: bfloat16 [32, 64, 96, 512], P('rows', 'cols'), may hold values from -0.078125 to 0.078125
- right_factors: bfloat16 [32, 64, 96, 512], P('rows', 'cols'), may hold values from -0.25 to 0.25
- ranks: int32 [32, 64], P('rows', 'cols'), may hold values from 8 to 96
- inputs: bfloat16 [32768, 256], P(('cols', 'rows')), may hold values from -6 to 6
- targets: bfloat16 [16384, 256], P(('rows', 'cols')), may hold values from -6 to 6
Outputs:
- gradient: float32 [32768, 256], P(('cols', 'rows'))
All inputs are finite; a program needn't handle non-finite values.
Results may differ from a plain program's by a relative error of at most 0.0073.
Values may be sent and summed in bfloat16 or wider, within the bound.
No kernel may reach another device: no remote copies, remote signals or barrier semaphores. Data moves between devices by JAX's collectives and lax.ppermute only.
A program may use at most 64 MiB of HBM per device.

v0:
```python
import jax
import jax.numpy as jnp
import numpy as np
from jax import lax
from jax.sharding import PartitionSpec as P


huber_scale = 1.0
CORES = 2


def grid_cycle(count):
    width = 1 << ((count.bit_length() - 1) // 2)
    depth = count // width
    if width % 2 or depth < 2 or depth * width != count:
        return list(range(count))
    places = []
    for x in range(width):
        run = range(1, depth) if x % 2 == 0 else range(depth - 1, 0, -1)
        places += [z * width + x for z in run]
    places += [x for x in range(width - 1, -1, -1)]
    return places


def pseudo_slope(residual):
    return (residual / jnp.sqrt(1.0 + jnp.square(residual / huber_scale))).astype(jnp.bfloat16)


def shards_of(tiles, count):
    number, width, size = tiles.shape
    if count >= number:
        parts = count // number
        cut = tiles.reshape(number, width, parts, size // parts).transpose(0, 2, 1, 3)
        return cut.reshape(count, width, size // parts)
    group = number // count
    cut = tiles.reshape(count, group, width, size).transpose(0, 2, 1, 3)
    return cut.reshape(count, width, group * size)


def tiles_of(shards, number, size):
    count, width, rows = shards.shape
    if count >= number:
        parts = count // number
        cut = shards.reshape(number, parts, width, rows).transpose(0, 2, 1, 3)
        return cut.reshape(number, width, size)
    group = number // count
    cut = shards.reshape(count, width, group, size).transpose(0, 2, 1, 3)
    return cut.reshape(number, width, size)


def solution(mesh):
    row_count, col_count = mesh.shape["rows"], mesh.shape["cols"]
    cores = CORES if row_count % CORES == 0 else 1
    y_count = row_count // cores
    half_way = col_count // 2
    cycle = grid_cycle(col_count)
    place_of = [cycle.index(c) for c in range(col_count)]
    ahead = [(cycle[p], cycle[(p + 1) % col_count]) for p in range(col_count)]
    behind = [(b, a) for a, b in ahead]
    core_swap = [(r, r - r % cores + (r + 1) % cores) for r in range(row_count)]
    y_next = [(r, (r + cores) % row_count) for r in range(row_count)]

    bits = 32 // col_count if col_count & (col_count - 1) == 0 else 0
    packed = bits > 0 and (1 << bits) >= col_count
    cycle_word = place_word = 0
    if packed:
        cycle_word = int(np.uint32(sum(c << (bits * p) for p, c in enumerate(cycle))).view(np.int32))
        place_word = int(np.uint32(sum(p << (bits * c) for c, p in enumerate(place_of))).view(np.int32))

    def columns_ahead(col):
        if not packed:
            table = [[cycle[(p + d) % col_count] for d in range(col_count)] for p in place_of]
            row = lax.dynamic_index_in_dim(jnp.asarray(table, jnp.int32), col, 0, False)
            return [row[d] for d in range(col_count)]
        low = (1 << bits) - 1
        shift = ((place_word_at(col)) & low) * bits
        word = lax.shift_right_logical(jnp.int32(cycle_word), shift) | (
            (jnp.int32(cycle_word) << (32 - bits - shift)) << bits
        )
        return [lax.shift_right_logical(word, jnp.int32(bits * d)) & low for d in range(col_count)]

    def place_word_at(col):
        return lax.shift_right_logical(jnp.int32(place_word), col * bits)

    def rows_back(row):
        if cores != 2 or row_count & (row_count - 1):
            y, core = row // cores, row % cores
            return [
                [((y - t) % y_count) * cores + (core + c) % cores for c in range(cores)]
                for t in range(y_count)
            ]
        back = [(row + (row_count - t * cores)) & (row_count - 1) if t else row for t in range(y_count)]
        return [[r, r ^ 1] for r in back]

    def on_device(left_factors, right_factors, ranks, inputs, targets):
        row_tiles, col_tiles, rank_cap, tile_size = left_factors.shape
        width = inputs.shape[1]
        group = col_tiles // row_count
        at = columns_ahead(lax.axis_index("cols"))
        first_tile = [[r * group for r in rows] for rows in rows_back(lax.axis_index("rows"))]
        one_tile = col_count == row_tiles
        wide = lambda block: block.astype(jnp.float32)
        narrow = lambda block: block.astype(jnp.bfloat16)
        window = lambda array, index, size, dim=0: lax.dynamic_slice_in_dim(
            array, index, size, dim, allow_negative_indices=False
        )
        pick = lambda array, index, dim=0: lax.squeeze(window(array, index, 1, dim), (dim,))
        put = lambda array, piece, index: lax.dynamic_update_slice_in_dim(
            array, piece, index, 0, allow_negative_indices=False
        )

        levels = jnp.arange(rank_cap, dtype=jnp.int32)
        active = levels[None, None, :] < ranks[:, :, None]

        def coefficients_of(factors, block, first, buffer):
            count = block.shape[0] // tile_size
            product = jnp.einsum(
                "ijrb,jbk->jirk",
                window(factors, first, count, 1),
                block.reshape(count, tile_size, width),
                preferred_element_type=jnp.float32,
            )
            mask = window(active, first, count, 1).transpose(1, 0, 2)
            product = narrow(jnp.where(mask[..., None], product, 0.0))
            return put(buffer, product, first)

        coefficient = jnp.zeros((col_tiles, row_tiles, rank_cap, width), jnp.bfloat16)
        mine = inputs
        for t in range(y_count):
            if t + 1 < y_count:
                following = lax.ppermute(mine, "rows", y_next)
            others = [mine]
            for _ in range(cores - 1):
                others.append(lax.ppermute(others[-1], "rows", core_swap))
            for c, other in enumerate(others):
                factors, other = lax.optimization_barrier((right_factors, other))
                coefficient = coefficients_of(factors, other, first_tile[t][c], coefficient)
            mine = following

        if one_tile:

            def part(d):
                tile = jnp.einsum(
                    "jrk,jrb->kb",
                    pick(coefficient, at[d], 1),
                    pick(left_factors, at[d]),
                    preferred_element_type=jnp.float32,
                )
                return lax.optimization_barrier(narrow(tile))

        else:
            shares = jnp.einsum(
                "ijrb,jirk->ikb", left_factors, coefficient, preferred_element_type=jnp.float32
            )
            shares = shards_of(narrow(shares), col_count)

            def part(d):
                return pick(shares, at[d])

        cut = width // 2
        far = part(half_way)
        up, down = far[:cut], far[cut:]
        for d in range(half_way - 1, -1, -1):
            up = lax.ppermute(up, "cols", ahead)
            down = lax.ppermute(down, "cols", behind)
            own_up = part(d)
            own_down = part(col_count - d) if d else None
            if up.shape[0] == cut:
                up = jnp.concatenate([wide(up), jnp.zeros(up.shape, jnp.float32)])
                down = jnp.concatenate([jnp.zeros(down.shape, jnp.float32), wide(down)])
            if d:
                up = narrow(wide(up) + wide(own_up))
                down = narrow(wide(down) + wide(own_down))
            else:
                total = wide(own_up) + wide(up) + wide(down)
        share_slopes = pseudo_slope(total - targets.T.astype(jnp.float32))

        if one_tile:

            def adjoint_of(block, d, buffer):
                product = jnp.einsum(
                    "jrb,kb->jrk", pick(left_factors, at[d]), block, preferred_element_type=jnp.float32
                )
                product = narrow(jnp.where(pick(active, at[d])[..., None], product, 0.0))
                return put(buffer, product[None], at[d])

            gathered = jnp.zeros((row_tiles, col_tiles, rank_cap, width), jnp.bfloat16)
        else:

            def adjoint_of(block, d, buffer):
                return put(buffer, block[None], at[d])

            gathered = jnp.zeros((col_count,) + share_slopes.shape, jnp.bfloat16)
        up = down = share_slopes
        held, places = [share_slopes], [0]
        for d in range(1, half_way + 1):
            if d == half_way:
                up, down = up[:cut], down[cut:]
            up = lax.ppermute(up, "cols", ahead)
            down = lax.ppermute(down, "cols", behind)
            for block, place in zip(held, places):
                gathered = adjoint_of(block, place, gathered)
            if d == half_way:
                held, places = [jnp.concatenate([up, down])], [half_way]
            else:
                held, places = [up, down], [col_count - d, d]
        for block, place in zip(held, places):
            gathered = adjoint_of(block, place, gathered)
        adjoint = gathered
        if not one_tile:
            adjoint = jnp.einsum(
                "ijrb,ikb->ijrk",
                left_factors,
                tiles_of(gathered, row_tiles, tile_size),
                preferred_element_type=jnp.float32,
            )
            adjoint = narrow(jnp.where(active[..., None], adjoint, 0.0))

        def terms(factors, values, t, c):
            first = first_tile[t % y_count][c]
            product = jnp.einsum(
                "ijrb,ijrk->jkb",
                window(factors, first, group, 1),
                window(values, first, group, 1),
                preferred_element_type=jnp.float32,
            )
            return lax.optimization_barrier(narrow(product))

        def chip_terms(factors, values, t):
            total = wide(terms(factors, values, t, 0))
            if cores > 1:
                other = terms(factors, values, t, 1)
                total = total + wide(lax.ppermute(other, "rows", core_swap))
            return total

        factors, values = lax.optimization_barrier((right_factors, adjoint))
        total = chip_terms(factors, values, 1)
        for t in range(2, y_count + 1):
            leaving, factors, values = lax.optimization_barrier((narrow(total), factors, values))
            moving = lax.ppermute(leaving, "rows", y_next)
            own = lax.optimization_barrier(chip_terms(factors, values, t))
            total = wide(moving) + own
        return total.transpose(0, 2, 1).reshape(group * tile_size, width)

    in_specs = (
        P("rows", "cols", None, None),
        P("rows", "cols", None, None),
        P("rows", "cols"),
        P(("cols", "rows"), None),
        P(("rows", "cols"), None),
    )
    out_specs = P(("cols", "rows"), None)
    return jax.shard_map(
        on_device, mesh=mesh, in_specs=in_specs, out_specs=out_specs, check_vma=False
    )
```

profile of v0, /device:TPU:0, one launch (start us, length us, event | category | flops | bytes accessed | tf_op | source)
XLA Modules:
  0.0 104.8 jit_solution(7163395464965331757)
XLA Ops:
  0.5 2.5 %collective-permute-start.1 = (bf16[1024,256]{1,0:T(8,128)(2,1)}, bf16[1024,256]{1,0:T(8,128)(2,1)}, u32[]{:S(2)}, u32[]{:S(2)}) collective-permute-start(bf16[1024,256]{1,0:T(8,128)(2,1)} %param.8), channel_id=1, source_target_pairs={{0,16},{8,24},{16,0},{24,8},{1,17},{9,25},{17,1},{25,9},{2,18},{10... | collective-permute-start | bytes 1572872 | tf_op jit(solution)/shard_map/ppermute | solution.py:131
  3.9 2.2 %select_convert_fusion.3 = bf16[2,8,96,256]{3,2,1,0:T(8,128)(2,1)S(1)} fusion(bf16[2,512,256,1]{2,1,3,0:T(8,128)(2,1)} %bitcast.249, s32[]{:T(128)S(6)} %mul.20, pred[2,8,96]{2,1,0:T(8,128)(4,1)S(1)} %copy.28, bf16[8,8,96,512]{3,2,1,0:T(8,128)(2,1)} %param.6), kind=kOutput, calls=%fused_computation.17 | convolution fusion | flops 403439616 | bytes 2885124 | tf_op jit(solution)/shard_map/ijrb,jbk->jirk/dot_general | solution.py:117
  6.6 9.3 %collective-permute-done.1 = bf16[1024,256]{1,0:T(8,128)(2,1)} collective-permute-done((bf16[1024,256]{1,0:T(8,128)(2,1)}, bf16[1024,256]{1,0:T(8,128)(2,1)}, u32[]{:S(2)}, u32[]{:S(2)}) %collective-permute-start.1) | collective-permute-done | bytes 524320 | tf_op jit(solution)/shard_map/ppermute | solution.py:131
  15.9 1.6 %select_convert_fusion.2 = bf16[2,8,96,256]{3,2,1,0:T(8,128)(2,1)S(1)} fusion(bf16[2,512,256,1]{2,1,3,0:T(8,128)(2,1)} %bitcast.9, s32[]{:T(128)S(6)} %mul.21, pred[2,8,96]{2,1,0:T(8,128)(4,1)S(1)} %copy.31, bf16[8,8,96,512]{3,2,1,0:T(8,128)(2,1)S(1)} %copy-done), kind=kOutput, calls=%fused_computation.14 | convolution fusion | flops 403439616 | bytes 2885636 | tf_op jit(solution)/shard_map/ijrb,jbk->jirk/dot_general | solution.py:117
  17.5 1.8 %select_convert_fusion.1 = bf16[2,8,96,256]{3,2,1,0:T(8,128)(2,1)S(1)} fusion(bf16[2,512,256,1]{2,1,3,0:T(8,128)(2,1)} %bitcast.13, s32[]{:T(128)S(6)} %mul.22, pred[2,8,96]{2,1,0:T(8,128)(4,1)S(1)} %copy.34, bf16[8,8,96,512]{3,2,1,0:T(8,128)(2,1)S(1)} %copy-done), kind=kOutput, calls=%fused_computation.11 | convolution fusion | flops 403439616 | bytes 2885636 | tf_op jit(solution)/shard_map/ijrb,jbk->jirk/dot_general | solution.py:117
  19.6 1.9 %collective-permute-done.2 = bf16[1024,256]{1,0:T(8,128)(2,1)S(1)} collective-permute-done((bf16[1024,256]{1,0:T(8,128)(2,1)}, bf16[1024,256]{1,0:T(8,128)(2,1)S(1)}, u32[]{:S(2)}, u32[]{:S(2)}) %collective-permute-start.2) | collective-permute-done | bytes 524320 | tf_op jit(solution)/shard_map/ppermute | solution.py:134
  22.6 1.9 %collective-permute-start.3 = (bf16[128,512]{1,0:T(8,128)(2,1)S(1)}, bf16[128,512]{1,0:T(8,128)(2,1)S(1)}, u32[]{:S(2)}, u32[]{:S(2)}) collective-permute-start(bf16[128,512]{1,0:T(8,128)(2,1)S(1)} %get-tuple-element.31), channel_id=1, source_target_pairs={{2,4},{4,6},{6,7},{7,5},{5,3},{3,1},{1,0},{0,2},{10,12},{12,14},{1... | collective-permute-start | bytes 393224 | tf_op jit(solution)/shard_map/ppermute | solution.py:164
  26.3 1.9 %collective-permute-done.3 = bf16[128,512]{1,0:T(8,128)(2,1)S(1)} collective-permute-done((bf16[128,512]{1,0:T(8,128)(2,1)S(1)}, bf16[128,512]{1,0:T(8,128)(2,1)S(1)}, u32[]{:S(2)}, u32[]{:S(2)}) %collective-permute-start.3) | collective-permute-done | bytes 131104 | tf_op jit(solution)/shard_map/ppermute | solution.py:164
  28.3 1.8 %collective-permute-start.4 = (bf16[256,512]{1,0:T(8,128)(2,1)S(1)}, bf16[256,512]{1,0:T(8,128)(2,1)S(1)}, u32[]{:S(2)}, u32[]{:S(2)}) collective-permute-start(bf16[256,512]{1,0:T(8,128)(2,1)S(1)} %add_convert_fusion.6), channel_id=1, source_target_pairs={{2,4},{4,6},{6,7},{7,5},{5,3},{3,1},{1,0},{0,2},{10,12},{12,14},{1... | collective-permute-start | bytes 786440 | tf_op jit(solution)/shard_map/ppermute | solution.py:164
  31.3 4.5 %collective-permute-done.4 = bf16[256,512]{1,0:T(8,128)(2,1)S(1)} collective-permute-done((bf16[256,512]{1,0:T(8,128)(2,1)S(1)}, bf16[256,512]{1,0:T(8,128)(2,1)S(1)}, u32[]{:S(2)}, u32[]{:S(2)}) %collective-permute-start.4) | collective-permute-done | bytes 262176 | tf_op jit(solution)/shard_map/ppermute | solution.py:164
  35.9 1.8 %collective-permute-start.5 = (bf16[256,512]{1,0:T(8,128)(2,1)S(1)}, bf16[256,512]{1,0:T(8,128)(2,1)S(1)}, u32[]{:S(2)}, u32[]{:S(2)}) collective-permute-start(bf16[256,512]{1,0:T(8,128)(2,1)S(1)} %add_convert_fusion.5), channel_id=1, source_target_pairs={{2,4},{4,6},{6,7},{7,5},{5,3},{3,1},{1,0},{0,2},{10,12},{12,14},{1... | collective-permute-start | bytes 786440 | tf_op jit(solution)/shard_map/ppermute | solution.py:164
  38.7 3.8 %collective-permute-done.5 = bf16[256,512]{1,0:T(8,128)(2,1)S(1)} collective-permute-done((bf16[256,512]{1,0:T(8,128)(2,1)S(1)}, bf16[256,512]{1,0:T(8,128)(2,1)S(1)}, u32[]{:S(2)}, u32[]{:S(2)}) %collective-permute-start.5) | collective-permute-done | bytes 262176 | tf_op jit(solution)/shard_map/ppermute | solution.py:164
  43.3 1.8 %collective-permute-start.6 = (bf16[256,512]{1,0:T(8,128)(2,1)}, bf16[256,512]{1,0:T(8,128)(2,1)}, u32[]{:S(2)}, u32[]{:S(2)}) collective-permute-start(bf16[256,512]{1,0:T(8,128)(2,1)} %add_convert_fusion.4), channel_id=1, source_target_pairs={{2,4},{4,6},{6,7},{7,5},{5,3},{3,1},{1,0},{0,2},{10,12},{12,14},{1... | collective-permute-start | bytes 786440 | tf_op jit(solution)/shard_map/ppermute | solution.py:164
  47.2 1.7 %fusion.72 = bf16[256,512]{1,0:T(8,128)(2,1)S(1)} fusion(bf16[8,8,96,512]{3,2,1,0:T(8,128)(2,1)} %param.5, s32[]{:T(128)S(6)} %and.33, bf16[8,8,96,256]{3,2,0,1:T(8,128)(2,1)S(1)} %copy_dynamic-update-slice_fusion), kind=kOutput, calls=%fused_computation.68 | convolution fusion | flops 201457664 | bytes 1442816 | tf_op jit(solution)/shard_map/jrk,jrb->kb/dot_general | solution.py:143
  50.0 2.6 %collective-permute-done.10 = bf16[256,512]{1,0:T(8,128)(2,1)} collective-permute-done((bf16[256,512]{1,0:T(8,128)(2,1)}, bf16[256,512]{1,0:T(8,128)(2,1)}, u32[]{:S(2)}, u32[]{:S(2)}) %collective-permute-start.10) | collective-permute-done | bytes 262176 | tf_op jit(solution)/shard_map/ppermute | solution.py:165
  52.6 1.2 %multiply_convert_fusion = bf16[256,512]{1,0:T(8,128)(2,1)S(1)} fusion(bf16[512,256]{0,1:T(8,128)(2,1)S(1)} %copy.40, bf16[256,512]{1,0:T(8,128)(2,1)} %collective-permute-done.10, bf16[256,512]{1,0:T(8,128)(2,1)} %collective-permute-done.6, bf16[256,512]{1,0:T(8,128)(2,1)S(1)} %fusion.72), kind=kLoop, calls=%fused_computation.120 | loop fusion | flops 1441792 | bytes 1310720 | tf_op jit(solution)/shard_map/convert_element_type | solution.py:26
  53.8 1.6 %collective-permute-start.11 = (bf16[256,512]{1,0:T(8,128)(2,1)S(1)}, bf16[256,512]{1,0:T(8,128)(2,1)S(1)}, u32[]{:S(2)}, u32[]{:S(2)}) collective-permute-start(bf16[256,512]{1,0:T(8,128)(2,1)S(1)} %multiply_convert_fusion), channel_id=1, source_target_pairs={{2,4},{4,6},{6,7},{7,5},{5,3},{3,1},{1,0},{0,2},{10,12},{12,14},{1... | collective-permute-start | bytes 786440 | tf_op jit(solution)/shard_map/ppermute | solution.py:199
  56.3 1.7 %fusion.71 = bf16[8,8,96,256]{3,2,0,1:T(8,128)(2,1)S(1)} fusion(bf16[8,8,96,256]{3,2,0,1:T(8,128)(2,1)S(1)} %broadcast.16, s32[]{:T(128)S(6)} %and.33, bf16[8,8,96,512]{3,2,1,0:T(8,128)(2,1)} %param.5, pred[8,96]{1,0:T(8,128)(4,1)S(1)} %get-tuple-element.40, bf16[256,512]{1,0:T(8,128)(2,1)S(1)} %multiply_convert_fusion), kind=kOutput, calls=%fused_computation.67 | convolution fusion | flops 201719808 | bytes 1443840 | tf_op jit(solution)/shard_map/jrb,kb->jrk/dot_general | solution.py:181
  58.0 4.3 %collective-permute-done.11 = bf16[256,512]{1,0:T(8,128)(2,1)S(1)} collective-permute-done((bf16[256,512]{1,0:T(8,128)(2,1)S(1)}, bf16[256,512]{1,0:T(8,128)(2,1)S(1)}, u32[]{:S(2)}, u32[]{:S(2)}) %collective-permute-start.11) | collective-permute-done | bytes 262176 | tf_op jit(solution)/shard_map/ppermute | solution.py:199
  62.4 1.6 %collective-permute-start.13 = (bf16[256,512]{1,0:T(8,128)(2,1)S(1)}, bf16[256,512]{1,0:T(8,128)(2,1)S(1)}, u32[]{:S(2)}, u32[]{:S(2)}) collective-permute-start(bf16[256,512]{1,0:T(8,128)(2,1)S(1)} %collective-permute-done.11), channel_id=1, source_target_pairs={{2,4},{4,6},{6,7},{7,5},{5,3},{3,1},{1,0},{0,2},{10,12},{12,14},{1... | collective-permute-start | bytes 786440 | tf_op jit(solution)/shard_map/ppermute | solution.py:199
  64.7 1.7 %fusion.69 = bf16[8,8,96,256]{3,2,0,1:T(8,128)(2,1)S(1)} fusion(bf16[8,8,96,256]{3,2,0,1:T(8,128)(2,1)S(1)} %fusion.71, s32[]{:T(128)S(6)} %and.41, bf16[8,8,96,512]{3,2,1,0:T(8,128)(2,1)} %param.5, pred[8,96]{1,0:T(8,128)(4,1)S(1)} %get-tuple-element.39, bf16[256,512]{1,0:T(8,128)(2,1)S(1)} %collective-permute-done.11), kind=kOutput, calls=%fused_computation.65 | convolution fusion | flops 201719808 | bytes 1443840 | tf_op jit(solution)/shard_map/jrb,kb->jrk/dot_general | solution.py:181
  66.3 1.5 %fusion.67 = bf16[8,8,96,256]{3,2,0,1:T(8,128)(2,1)S(1)} fusion(bf16[8,8,96,256]{3,2,0,1:T(8,128)(2,1)S(1)} %fusion.69, s32[]{:T(128)S(6)} %and.38, bf16[8,8,96,512]{3,2,1,0:T(8,128)(2,1)} %param.5, pred[8,96]{1,0:T(8,128)(4,1)S(1)} %get-tuple-element.38, bf16[256,512]{1,0:T(8,128)(2,1)S(1)} %collective-permute-done.12), kind=kOutput, calls=%fused_computation.63 | convolution fusion | flops 201719808 | bytes 1443840 | tf_op jit(solution)/shard_map/jrb,kb->jrk/dot_general | solution.py:181
  67.9 3.5 %collective-permute-done.13 = bf16[256,512]{1,0:T(8,128)(2,1)S(1)} collective-permute-done((bf16[256,512]{1,0:T(8,128)(2,1)S(1)}, bf16[256,512]{1,0:T(8,128)(2,1)S(1)}, u32[]{:S(2)}, u32[]{:S(2)}) %collective-permute-start.13) | collective-permute-done | bytes 262176 | tf_op jit(solution)/shard_map/ppermute | solution.py:199
  71.4 1.6 %collective-permute-start.15 = (bf16[256,512]{1,0:T(8,128)(2,1)S(1)}, bf16[256,512]{1,0:T(8,128)(2,1)S(1)}, u32[]{:S(2)}, u32[]{:S(2)}) collective-permute-start(bf16[256,512]{1,0:T(8,128)(2,1)S(1)} %collective-permute-done.13), channel_id=1, source_target_pairs={{2,4},{4,6},{6,7},{7,5},{5,3},{3,1},{1,0},{0,2},{10,12},{12,14},{1... | collective-permute-start | bytes 786440 | tf_op jit(solution)/shard_map/ppermute | solution.py:199
  74.2 4.0 %collective-permute-done.15 = bf16[256,512]{1,0:T(8,128)(2,1)S(1)} collective-permute-done((bf16[256,512]{1,0:T(8,128)(2,1)S(1)}, bf16[256,512]{1,0:T(8,128)(2,1)S(1)}, u32[]{:S(2)}, u32[]{:S(2)}) %collective-permute-start.15) | collective-permute-done | bytes 262176 | tf_op jit(solution)/shard_map/ppermute | solution.py:199
  78.2 1.6 %collective-permute-start.17 = (bf16[128,512]{1,0:T(8,128)(2,1)S(1)}, bf16[128,512]{1,0:T(8,128)(2,1)S(1)}, u32[]{:S(2)}, u32[]{:S(2)}) collective-permute-start(bf16[128,512]{1,0:T(8,128)(2,1)S(1)} %slice.18), channel_id=1, source_target_pairs={{2,4},{4,6},{6,7},{7,5},{5,3},{3,1},{1,0},{0,2},{10,12},{12,14},{1... | collective-permute-start | bytes 393224 | tf_op jit(solution)/shard_map/ppermute | solution.py:199
  81.3 1.9 %collective-permute-done.17 = bf16[128,512]{1,0:T(8,128)(2,1)S(1)} collective-permute-done((bf16[128,512]{1,0:T(8,128)(2,1)S(1)}, bf16[128,512]{1,0:T(8,128)(2,1)S(1)}, u32[]{:S(2)}, u32[]{:S(2)}) %collective-permute-start.17) | collective-permute-done | bytes 131104 | tf_op jit(solution)/shard_map/ppermute | solution.py:199
  83.2 1.8 %collective-permute-done.18 = bf16[128,512]{1,0:T(8,128)(2,1)S(1)} collective-permute-done((bf16[128,512]{1,0:T(8,128)(2,1)S(1)}, bf16[128,512]{1,0:T(8,128)(2,1)S(1)}, u32[]{:S(2)}, u32[]{:S(2)}) %collective-permute-start.18) | collective-permute-done | bytes 131104 | tf_op jit(solution)/shard_map/ppermute | solution.py:200
  86.8 1.3 %collective-permute-done.19 = bf16[2,256,512]{2,1,0:T(8,128)(2,1)S(1)} collective-permute-done((bf16[2,256,512]{2,1,0:T(8,128)(2,1)S(1)}, bf16[2,256,512]{2,1,0:T(8,128)(2,1)S(1)}, u32[]{:S(2)}, u32[]{:S(2)}) %collective-permute-start.19) | collective-permute-done | bytes 524320 | tf_op jit(solution)/shard_map/ppermute | solution.py:233
  89.1 1.5 %collective-permute-start.20 = (bf16[2,256,512]{2,1,0:T(8,128)(2,1)S(1)}, bf16[2,256,512]{2,1,0:T(8,128)(2,1)S(1)}, u32[]{:S(2)}, u32[]{:S(2)}) collective-permute-start(bf16[2,256,512]{2,1,0:T(8,128)(2,1)S(1)} %add_convert_fusion), channel_id=1, source_target_pairs={{0,16},{8,24},{16,0},{24,8},{1,17},{9,25},{17,1},{25,9},{2,18},{10... | collective-permute-start | bytes 1572872 | tf_op jit(solution)/shard_map/ppermute | solution.py:240
  91.4 11.9 %collective-permute-done.20 = bf16[2,256,512]{2,1,0:T(8,128)(2,1)S(1)} collective-permute-done((bf16[2,256,512]{2,1,0:T(8,128)(2,1)S(1)}, bf16[2,256,512]{2,1,0:T(8,128)(2,1)S(1)}, u32[]{:S(2)}, u32[]{:S(2)}) %collective-permute-start.20) | collective-permute-done | bytes 524320 | tf_op jit(solution)/shard_map/ppermute | solution.py:240
  103.5 1.3 %copy.53 = f32[2,512,256]{2,1,0:T(8,128)} copy(f32[2,512,256]{1,2,0:T(8,128)S(1)} %add_bitcast_fusion) | data formatting | bytes 2097152 | tf_op jit(solution)/shard_map/transpose | solution.py:243
  (81 shorter events, 19.2 us)
Async XLA Ops:
  0.0 6.6 %collective-permute-start = (bf16[1024,256]{1,0:T(8,128)(2,1)}, bf16[1024,256]{1,0:T(8,128)(2,1)}, u32[]{:S(2)}, u32[]{:S(2)}) collective-permute-start(bf16[1024,256]{1,0:T(8,128)(2,1)} %param.8), channel_id=1, source_target_pairs={{0,8},{8,0},{16,24},{24,16},{1,9},{9,1},{17,25},{25,17},{2,10},{10... | collective-permute-start | bytes 1572872 | tf_op jit(solution)/shard_map/ppermute | solution.py:134
  0.5 15.4 %collective-permute-start.1 = (bf16[1024,256]{1,0:T(8,128)(2,1)}, bf16[1024,256]{1,0:T(8,128)(2,1)}, u32[]{:S(2)}, u32[]{:S(2)}) collective-permute-start(bf16[1024,256]{1,0:T(8,128)(2,1)} %param.8), channel_id=1, source_target_pairs={{0,16},{8,24},{16,0},{24,8},{1,17},{9,25},{17,1},{25,9},{2,18},{10... | collective-permute-start | bytes 1572872 | tf_op jit(solution)/shard_map/ppermute | solution.py:131
  3.9 12.0 %copy-start = (bf16[8,8,96,512]{3,2,1,0:T(8,128)(2,1)S(1)}, bf16[8,8,96,512]{3,2,1,0:T(8,128)(2,1)}, u32[]{:S(2)}) copy-start(bf16[8,8,96,512]{3,2,1,0:T(8,128)(2,1)} %param.6) | copy-start | bytes 18874372
  17.5 4.6 %slice-start = ((s8[6291456]{0:T(1024)(128)(4,1)}), s8[4194304]{0:T(1024)(128)(4,1)S(1)}, s32[]{:S(2)}) async-start(s8[6291456]{0:T(1024)(128)(4,1)} %bitcast.243), calls=%async_computation | async-start | bytes 8388608
  19.3 2.2 %collective-permute-start.2 = (bf16[1024,256]{1,0:T(8,128)(2,1)}, bf16[1024,256]{1,0:T(8,128)(2,1)S(1)}, u32[]{:S(2)}, u32[]{:S(2)}) collective-permute-start(bf16[1024,256]{1,0:T(8,128)(2,1)} %collective-permute-done.1), channel_id=1, source_target_pairs={{0,8},{8,0},{16,24},{24,16},{1,9},{9,1},{17,25},{25,17},{2,10},{10... | collective-permute-start | bytes 1572872 | tf_op jit(solution)/shard_map/ppermute | solution.py:134
  19.5 2.7 %slice-start.1 = ((s8[6291456]{0:T(1024)(128)(4,1)}), s8[2097152]{0:T(1024)(128)(4,1)S(1)}, s32[]{:S(2)}) async-start(s8[6291456]{0:T(1024)(128)(4,1)} %bitcast.243), calls=%async_computation.1 | async-start | bytes 4194304
  22.6 5.6 %collective-permute-start.3 = (bf16[128,512]{1,0:T(8,128)(2,1)S(1)}, bf16[128,512]{1,0:T(8,128)(2,1)S(1)}, u32[]{:S(2)}, u32[]{:S(2)}) collective-permute-start(bf16[128,512]{1,0:T(8,128)(2,1)S(1)} %get-tuple-element.31), channel_id=1, source_target_pairs={{2,4},{4,6},{6,7},{7,5},{5,3},{3,1},{1,0},{0,2},{10,12},{12,14},{1... | collective-permute-start | bytes 393224 | tf_op jit(solution)/shard_map/ppermute | solution.py:164
  25.3 5.3 %collective-permute-start.7 = (bf16[128,512]{1,0:T(8,128)(2,1)S(1)}, bf16[128,512]{1,0:T(8,128)(2,1)S(1)}, u32[]{:S(2)}, u32[]{:S(2)}) collective-permute-start(bf16[128,512]{1,0:T(8,128)(2,1)S(1)} %get-tuple-element.32), channel_id=1, source_target_pairs={{4,2},{6,4},{7,6},{5,7},{3,5},{1,3},{0,1},{2,0},{12,10},{14,12},{1... | collective-permute-start | bytes 393224 | tf_op jit(solution)/shard_map/ppermute | solution.py:165
  28.3 7.5 %collective-permute-start.4 = (bf16[256,512]{1,0:T(8,128)(2,1)S(1)}, bf16[256,512]{1,0:T(8,128)(2,1)S(1)}, u32[]{:S(2)}, u32[]{:S(2)}) collective-permute-start(bf16[256,512]{1,0:T(8,128)(2,1)S(1)} %add_convert_fusion.6), channel_id=1, source_target_pairs={{2,4},{4,6},{6,7},{7,5},{5,3},{3,1},{1,0},{0,2},{10,12},{12,14},{1... | collective-permute-start | bytes 786440 | tf_op jit(solution)/shard_map/ppermute | solution.py:164
  30.6 7.3 %collective-permute-start.8 = (bf16[256,512]{1,0:T(8,128)(2,1)S(1)}, bf16[256,512]{1,0:T(8,128)(2,1)S(1)}, u32[]{:S(2)}, u32[]{:S(2)}) collective-permute-start(bf16[256,512]{1,0:T(8,128)(2,1)S(1)} %add_convert_fusion.3), channel_id=1, source_target_pairs={{4,2},{6,4},{7,6},{5,7},{3,5},{1,3},{0,1},{2,0},{12,10},{14,12},{1... | collective-permute-start | bytes 786440 | tf_op jit(solution)/shard_map/ppermute | solution.py:165
  35.9 6.7 %collective-permute-start.5 = (bf16[256,512]{1,0:T(8,128)(2,1)S(1)}, bf16[256,512]{1,0:T(8,128)(2,1)S(1)}, u32[]{:S(2)}, u32[]{:S(2)}) collective-permute-start(bf16[256,512]{1,0:T(8,128)(2,1)S(1)} %add_convert_fusion.5), channel_id=1, source_target_pairs={{2,4},{4,6},{6,7},{7,5},{5,3},{3,1},{1,0},{0,2},{10,12},{12,14},{1... | collective-permute-start | bytes 786440 | tf_op jit(solution)/shard_map/ppermute | solution.py:164
  37.9 7.2 %collective-permute-start.9 = (bf16[256,512]{1,0:T(8,128)(2,1)S(1)}, bf16[256,512]{1,0:T(8,128)(2,1)S(1)}, u32[]{:S(2)}, u32[]{:S(2)}) collective-permute-start(bf16[256,512]{1,0:T(8,128)(2,1)S(1)} %add_convert_fusion.2), channel_id=1, source_target_pairs={{4,2},{6,4},{7,6},{5,7},{3,5},{1,3},{0,1},{2,0},{12,10},{14,12},{1... | collective-permute-start | bytes 786440 | tf_op jit(solution)/shard_map/ppermute | solution.py:165
  43.3 6.7 %collective-permute-start.6 = (bf16[256,512]{1,0:T(8,128)(2,1)}, bf16[256,512]{1,0:T(8,128)(2,1)}, u32[]{:S(2)}, u32[]{:S(2)}) collective-permute-start(bf16[256,512]{1,0:T(8,128)(2,1)} %add_convert_fusion.4), channel_id=1, source_target_pairs={{2,4},{4,6},{6,7},{7,5},{5,3},{3,1},{1,0},{0,2},{10,12},{12,14},{1... | collective-permute-start | bytes 786440 | tf_op jit(solution)/shard_map/ppermute | solution.py:164
  45.9 6.7 %collective-permute-start.10 = (bf16[256,512]{1,0:T(8,128)(2,1)}, bf16[256,512]{1,0:T(8,128)(2,1)}, u32[]{:S(2)}, u32[]{:S(2)}) collective-permute-start(bf16[256,512]{1,0:T(8,128)(2,1)} %add_convert_fusion.1), channel_id=1, source_target_pairs={{4,2},{6,4},{7,6},{5,7},{3,5},{1,3},{0,1},{2,0},{12,10},{14,12},{1... | collective-permute-start | bytes 786440 | tf_op jit(solution)/shard_map/ppermute | solution.py:165
  47.2 26.2 %slice-start.2 = ((s8[6291456]{0:T(1024)(128)(4,1)}), s8[4194304]{0:T(1024)(128)(4,1)S(1)}, s32[]{:S(2)}) async-start(s8[6291456]{0:T(1024)(128)(4,1)} %bitcast.245), calls=%async_computation.2 | async-start | bytes 8388608
  53.8 8.5 %collective-permute-start.11 = (bf16[256,512]{1,0:T(8,128)(2,1)S(1)}, bf16[256,512]{1,0:T(8,128)(2,1)S(1)}, u32[]{:S(2)}, u32[]{:S(2)}) collective-permute-start(bf16[256,512]{1,0:T(8,128)(2,1)S(1)} %multiply_convert_fusion), channel_id=1, source_target_pairs={{2,4},{4,6},{6,7},{7,5},{5,3},{3,1},{1,0},{0,2},{10,12},{12,14},{1... | collective-permute-start | bytes 786440 | tf_op jit(solution)/shard_map/ppermute | solution.py:199
  55.4 8.8 %collective-permute-start.12 = (bf16[256,512]{1,0:T(8,128)(2,1)S(1)}, bf16[256,512]{1,0:T(8,128)(2,1)S(1)}, u32[]{:S(2)}, u32[]{:S(2)}) collective-permute-start(bf16[256,512]{1,0:T(8,128)(2,1)S(1)} %multiply_convert_fusion), channel_id=1, source_target_pairs={{4,2},{6,4},{7,6},{5,7},{3,5},{1,3},{0,1},{2,0},{12,10},{14,12},{1... | collective-permute-start | bytes 786440 | tf_op jit(solution)/shard_map/ppermute | solution.py:200
  55.9 17.5 %slice-start.3 = ((s8[6291456]{0:T(1024)(128)(4,1)}), s8[2097152]{0:T(1024)(128)(4,1)S(1)}, s32[]{:S(2)}) async-start(s8[6291456]{0:T(1024)(128)(4,1)} %bitcast.245), calls=%async_computation.3 | async-start | bytes 4194304
  62.4 9.0 %collective-permute-start.13 = (bf16[256,512]{1,0:T(8,128)(2,1)S(1)}, bf16[256,512]{1,0:T(8,128)(2,1)S(1)}, u32[]{:S(2)}, u32[]{:S(2)}) collective-permute-start(bf16[256,512]{1,0:T(8,128)(2,1)S(1)} %collective-permute-done.11), channel_id=1, source_target_pairs={{2,4},{4,6},{6,7},{7,5},{5,3},{3,1},{1,0},{0,2},{10,12},{12,14},{1... | collective-permute-start | bytes 786440 | tf_op jit(solution)/shard_map/ppermute | solution.py:199
  64.2 8.7 %collective-permute-start.14 = (bf16[256,512]{1,0:T(8,128)(2,1)S(1)}, bf16[256,512]{1,0:T(8,128)(2,1)S(1)}, u32[]{:S(2)}, u32[]{:S(2)}) collective-permute-start(bf16[256,512]{1,0:T(8,128)(2,1)S(1)} %collective-permute-done.12), channel_id=1, source_target_pairs={{4,2},{6,4},{7,6},{5,7},{3,5},{1,3},{0,1},{2,0},{12,10},{14,12},{1... | collective-permute-start | bytes 786440 | tf_op jit(solution)/shard_map/ppermute | solution.py:200
  64.7 20.8 %slice-start.4 = ((s8[6291456]{0:T(1024)(128)(4,1)}), s8[2097152]{0:T(1024)(128)(4,1)S(1)}, s32[]{:S(2)}) async-start(s8[6291456]{0:T(1024)(128)(4,1)} %bitcast.247), calls=%async_computation.4 | async-start | bytes 4194304
  71.4 6.8 %collective-permute-start.15 = (bf16[256,512]{1,0:T(8,128)(2,1)S(1)}, bf16[256,512]{1,0:T(8,128)(2,1)S(1)}, u32[]{:S(2)}, u32[]{:S(2)}) collective-permute-start(bf16[256,512]{1,0:T(8,128)(2,1)S(1)} %collective-permute-done.13), channel_id=1, source_target_pairs={{2,4},{4,6},{6,7},{7,5},{5,3},{3,1},{1,0},{0,2},{10,12},{12,14},{1... | collective-permute-start | bytes 786440 | tf_op jit(solution)/shard_map/ppermute | solution.py:199
  72.9 6.9 %collective-permute-start.16 = (bf16[256,512]{1,0:T(8,128)(2,1)S(1)}, bf16[256,512]{1,0:T(8,128)(2,1)S(1)}, u32[]{:S(2)}, u32[]{:S(2)}) collective-permute-start(bf16[256,512]{1,0:T(8,128)(2,1)S(1)} %collective-permute-done.14), channel_id=1, source_target_pairs={{4,2},{6,4},{7,6},{5,7},{3,5},{1,3},{0,1},{2,0},{12,10},{14,12},{1... | collective-permute-start | bytes 786440 | tf_op jit(solution)/shard_map/ppermute | solution.py:200
  73.8 11.6 %slice-start.5 = ((s8[6291456]{0:T(1024)(128)(4,1)}), s8[4194304]{0:T(1024)(128)(4,1)S(1)}, s32[]{:S(2)}) async-start(s8[6291456]{0:T(1024)(128)(4,1)} %bitcast.247), calls=%async_computation.5 | async-start | bytes 8388608
  78.2 5.0 %collective-permute-start.17 = (bf16[128,512]{1,0:T(8,128)(2,1)S(1)}, bf16[128,512]{1,0:T(8,128)(2,1)S(1)}, u32[]{:S(2)}, u32[]{:S(2)}) collective-permute-start(bf16[128,512]{1,0:T(8,128)(2,1)S(1)} %slice.18), channel_id=1, source_target_pairs={{2,4},{4,6},{6,7},{7,5},{5,3},{3,1},{1,0},{0,2},{10,12},{12,14},{1... | collective-permute-start | bytes 393224 | tf_op jit(solution)/shard_map/ppermute | solution.py:199
  79.8 5.2 %collective-permute-start.18 = (bf16[128,512]{1,0:T(8,128)(2,1)S(1)}, bf16[128,512]{1,0:T(8,128)(2,1)S(1)}, u32[]{:S(2)}, u32[]{:S(2)}) collective-permute-start(bf16[128,512]{1,0:T(8,128)(2,1)S(1)} %slice.19), channel_id=1, source_target_pairs={{4,2},{6,4},{7,6},{5,7},{3,5},{1,3},{0,1},{2,0},{12,10},{14,12},{1... | collective-permute-start | bytes 393224 | tf_op jit(solution)/shard_map/ppermute | solution.py:200
  86.1 2.0 %collective-permute-start.19 = (bf16[2,256,512]{2,1,0:T(8,128)(2,1)S(1)}, bf16[2,256,512]{2,1,0:T(8,128)(2,1)S(1)}, u32[]{:S(2)}, u32[]{:S(2)}) collective-permute-start(bf16[2,256,512]{2,1,0:T(8,128)(2,1)S(1)} %fusion.42), channel_id=1, source_target_pairs={{0,8},{8,0},{16,24},{24,16},{1,9},{9,1},{17,25},{25,17},{2,10},{10... | collective-permute-start | bytes 1572872 | tf_op jit(solution)/shard_map/ppermute | solution.py:233
  88.9 2.4 %collective-permute-start.21 = (bf16[2,256,512]{2,1,0:T(8,128)(2,1)S(1)}, bf16[2,256,512]{2,1,0:T(8,128)(2,1)S(1)}, u32[]{:S(2)}, u32[]{:S(2)}) collective-permute-start(bf16[2,256,512]{2,1,0:T(8,128)(2,1)S(1)} %fusion.36), channel_id=1, source_target_pairs={{0,8},{8,0},{16,24},{24,16},{1,9},{9,1},{17,25},{25,17},{2,10},{10... | collective-permute-start | bytes 1572872 | tf_op jit(solution)/shard_map/ppermute | solution.py:233
  89.1 14.2 %collective-permute-start.20 = (bf16[2,256,512]{2,1,0:T(8,128)(2,1)S(1)}, bf16[2,256,512]{2,1,0:T(8,128)(2,1)S(1)}, u32[]{:S(2)}, u32[]{:S(2)}) collective-permute-start(bf16[2,256,512]{2,1,0:T(8,128)(2,1)S(1)} %add_convert_fusion), channel_id=1, source_target_pairs={{0,16},{8,24},{16,0},{24,8},{1,17},{9,25},{17,1},{25,9},{2,18},{10... | collective-permute-start | bytes 1572872 | tf_op jit(solution)/shard_map/ppermute | solution.py:240
where the time goes:
time: 105 us
  waiting for transfers between devices  54.6 us (52%)
  starting transfers between devices  21.9 us (21%)
  matrix products  20 us (19%)
  other arithmetic  4.21 us (4%)
  local copies, waits for them, and re-layouts  3.59 us (3%)
    ppermute x8, waiting for transfers between devices, on_device(): up = lax.ppermute(up, 'cols', ahead)  24.9 us
    ppermute x8, starting transfers between devices, on_device(): up = lax.ppermute(up, 'cols', ahead)  13.7 us
    ppermute x1, waiting for transfers between devices, on_device(): moving = lax.ppermute(leaving, 'rows', y_next)  11.9 us
    ppermute x1, waiting for transfers between devices, on_device(): following = lax.ppermute(mine, 'rows', y_next)  9.3 us
    dot_general x8, matrix products, adjoint_of(): jnp.einsum('jrb,kb->jrk', pick(left_factors, at[d]), block, preferred_ele...  6.93 us
    dot_general x4, matrix products, coefficients_of(): jnp.einsum('ijrb,jbk->jirk', window(factors, first, count, 1), block.resh...  6.19 us
    ppermute x8, waiting for transfers between devices, on_device(): down = lax.ppermute(down, 'cols', behind)  5.29 us
    dot_general x8, matrix products, part(): jnp.einsum('jrk,jrb->kb', pick(coefficient, at[d], 1), pick(left_factors,...  4.39 us
  transfers between devices with their start and end apart: 22, of which 17 were waited for; matrix products, arithmetic and copies ran while one was open for 18% of the time, Pallas kernels for 0%

commit v1 on v0

--- a/solution.py
+++ b/solution.py
@@ -2,6 +2,8 @@
 import jax.numpy as jnp
 import numpy as np
 from jax import lax
+from jax.experimental import pallas as pl
+from jax.experimental.pallas import tpu as pltpu
 from jax.sharding import PartitionSpec as P
 
 
@@ -26,6 +28,19 @@
     return (residual / jnp.sqrt(1.0 + jnp.square(residual / huber_scale))).astype(jnp.bfloat16)
 
 
+def turned(block):
+    def turn(source, target):
+        target[...] = source[...].T
+
+    rows, width = block.shape
+    return pl.pallas_call(
+        turn,
+        out_shape=jax.ShapeDtypeStruct((width, rows), block.dtype),
+        compiler_params=pltpu.CompilerParams(vmem_limit_bytes=4 << 20),
+        name="turned",
+    )(block)
+
+
 def shards_of(tiles, count):
     number, width, size = tiles.shape
     if count >= number:
@@ -77,7 +92,9 @@
         word = lax.shift_right_logical(jnp.int32(cycle_word), shift) | (
             (jnp.int32(cycle_word) << (32 - bits - shift)) << bits
         )
-        return [lax.shift_right_logical(word, jnp.int32(bits * d)) & low for d in range(col_count)]
+        return [col] + [
+            lax.shift_right_logical(word, jnp.int32(bits * d)) & low for d in range(1, col_count)
+        ]
 
     def place_word_at(col):
         return lax.shift_right_logical(jnp.int32(place_word), col * bits)
@@ -109,6 +126,8 @@
             array, piece, index, 0, allow_negative_indices=False
         )
 
+        goal = turned(targets)
+
         levels = jnp.arange(rank_cap, dtype=jnp.int32)
         active = levels[None, None, :] < ranks[:, :, None]
 
@@ -173,7 +192,7 @@
                 down = narrow(wide(down) + wide(own_down))
             else:
                 total = wide(own_up) + wide(up) + wide(down)
-        share_slopes = pseudo_slope(total - targets.T.astype(jnp.float32))
+        share_slopes = pseudo_slope(total - wide(goal))
 
         if one_tile:
 

time: 105 us -> 99.8 us (0.950)
  matrix products: 20 us -> 12.7 us
  waiting for transfers between devices: 54.6 us -> 60 us
  other arithmetic: 4.21 us -> 1.78 us
  local copies, waits for them, and re-layouts: 3.59 us -> 2.48 us
    ppermute x8, waiting for transfers between devices: 24.9 us -> 31.2 us  [on_device(): up = lax.ppermute(up, 'cols', ahead)]
    dot_general x8, matrix products: 6.93 us -> 3.17 us  [adjoint_of(): jnp.einsum('jrb,kb->jrk', pick(left_factors, at[d]), block, preferred_ele...]
    dot_general x4, matrix products: 6.19 us -> 3.96 us  [coefficients_of(): jnp.einsum('ijrb,jbk->jirk', window(factors, first, count, 1), block.resh...]
    convert_element_type x7, other arithmetic: 1.88 us -> 0.47 us  [on_device(): narrow = lambda block: block.astype(jnp.bfloat16)]
    dot_general x8, matrix products: 4.39 us -> 3.1 us  [part(): jnp.einsum('jrk,jrb->kb', pick(coefficient, at[d], 1), pick(left_factors,...]
    unnamed x15 -> x8, local copies, waits for them, and re-layouts: 1.14 us -> 0.03 us
  transfers between devices with their start and end apart: 22 -> 22, of which waited for: 17 -> 17; matrix products, arithmetic and copies ran while one was open for 18% -> 11% of each run, Pallas kernels for 0% -> 0%
where the time goes in v1:
time: 99.8 us; the launch traced here: 99.6 us
  waiting for transfers between devices  60 us (60%)
  starting transfers between devices  22 us (22%)
  matrix products  12.7 us (13%)
  local copies, waits for them, and re-layouts  2.48 us (2%)
  other arithmetic  1.78 us (2%)
    ppermute x8, waiting for transfers between devices, on_device(): up = lax.ppermute(up, 'cols', ahead)  31.2 us
    ppermute x8, starting transfers between devices, on_device(): up = lax.ppermute(up, 'cols', ahead)  13.8 us
    ppermute x1, waiting for transfers between devices, on_device(): moving = lax.ppermute(leaving, 'rows', y_next)  11.9 us
    ppermute x1, waiting for transfers between devices, on_device(): following = lax.ppermute(mine, 'rows', y_next)  9.19 us
    ppermute x8, waiting for transfers between devices, on_device(): down = lax.ppermute(down, 'cols', behind)  4.68 us
    dot_general x4, matrix products, coefficients_of(): jnp.einsum('ijrb,jbk->jirk', window(factors, first, count, 1), block.resh...  3.96 us
    ppermute x8, starting transfers between devices, on_device(): down = lax.ppermute(down, 'cols', behind)  3.37 us
    dot_general x8, matrix products, adjoint_of(): jnp.einsum('jrb,kb->jrk', pick(left_factors, at[d]), block, preferred_ele...  3.17 us
  transfers between devices with their start and end apart: 22, of which 17 were waited for; matrix products, arithmetic and copies ran while one was open for 11% of the time, Pallas kernels for 0%

profile of v1, /device:TPU:0, one launch (start us, length us, event | category | flops | bytes accessed | tf_op | source)
XLA Modules:
  0.0 99.6 jit_solution(5287445327470538749)
XLA Ops:
  0.5 2.5 %collective-permute-start.1 = (bf16[1024,256]{1,0:T(8,128)(2,1)}, bf16[1024,256]{1,0:T(8,128)(2,1)S(1)}, u32[]{:S(2)}, u32[]{:S(2)}) collective-permute-start(bf16[1024,256]{1,0:T(8,128)(2,1)} %param.8), channel_id=1, source_target_pairs={{0,16},{8,24},{16,0},{24,8},{1,17},{9,25},{17,1},{25,9},{2,18},{10... | collective-permute-start | bytes 1572872 | tf_op jit(solution)/shard_map/ppermute | solution.py:150
  3.0 0.8 iota_compare_fusion
  3.9 2.2 %select_convert_fusion.3 = bf16[2,8,96,256]{3,2,1,0:T(8,128)(2,1)S(1)} fusion(bf16[2,512,256,1]{2,1,3,0:T(8,128)(2,1)} %bitcast.241, s32[]{:T(128)S(6)} %mul.18, pred[2,8,96]{2,1,0:T(8,128)(4,1)S(1)} %copy.27, bf16[8,8,96,512]{3,2,1,0:T(8,128)(2,1)} %param.6), kind=kOutput, calls=%fused_computation.17 | convolution fusion | flops 403439616 | bytes 2885124 | tf_op jit(solution)/shard_map/ijrb,jbk->jirk/dot_general | solution.py:136
  6.6 9.2 %collective-permute-done.1 = bf16[1024,256]{1,0:T(8,128)(2,1)S(1)} collective-permute-done((bf16[1024,256]{1,0:T(8,128)(2,1)}, bf16[1024,256]{1,0:T(8,128)(2,1)S(1)}, u32[]{:S(2)}, u32[]{:S(2)}) %collective-permute-start.1) | collective-permute-done | bytes 524320 | tf_op jit(solution)/shard_map/ppermute | solution.py:150
  17.2 1.7 %collective-permute-done.2 = bf16[1024,256]{1,0:T(8,128)(2,1)S(1)} collective-permute-done((bf16[1024,256]{1,0:T(8,128)(2,1)S(1)}, bf16[1024,256]{1,0:T(8,128)(2,1)S(1)}, u32[]{:S(2)}, u32[]{:S(2)}) %collective-permute-start.2) | collective-permute-done | bytes 524320 | tf_op jit(solution)/shard_map/ppermute | solution.py:153
  20.1 1.8 %collective-permute-start.3 = (bf16[128,512]{1,0:T(8,128)(2,1)S(1)}, bf16[128,512]{1,0:T(8,128)(2,1)S(1)}, u32[]{:S(2)}, u32[]{:S(2)}) collective-permute-start(bf16[128,512]{1,0:T(8,128)(2,1)S(1)} %get-tuple-element.31), channel_id=1, source_target_pairs={{2,4},{4,6},{6,7},{7,5},{5,3},{3,1},{1,0},{0,2},{10,12},{12,14},{1... | collective-permute-start | bytes 393224 | tf_op jit(solution)/shard_map/ppermute | solution.py:183
  23.8 1.9 %collective-permute-done.3 = bf16[128,512]{1,0:T(8,128)(2,1)S(1)} collective-permute-done((bf16[128,512]{1,0:T(8,128)(2,1)S(1)}, bf16[128,512]{1,0:T(8,128)(2,1)S(1)}, u32[]{:S(2)}, u32[]{:S(2)}) %collective-permute-start.3) | collective-permute-done | bytes 131104 | tf_op jit(solution)/shard_map/ppermute | solution.py:183
  25.7 1.8 %collective-permute-start.4 = (bf16[256,512]{1,0:T(8,128)(2,1)S(1)}, bf16[256,512]{1,0:T(8,128)(2,1)S(1)}, u32[]{:S(2)}, u32[]{:S(2)}) collective-permute-start(bf16[256,512]{1,0:T(8,128)(2,1)S(1)} %add_convert_fusion.6), channel_id=1, source_target_pairs={{2,4},{4,6},{6,7},{7,5},{5,3},{3,1},{1,0},{0,2},{10,12},{12,14},{1... | collective-permute-start | bytes 786440 | tf_op jit(solution)/shard_map/ppermute | solution.py:183
  28.8 4.4 %collective-permute-done.4 = bf16[256,512]{1,0:T(8,128)(2,1)S(1)} collective-permute-done((bf16[256,512]{1,0:T(8,128)(2,1)S(1)}, bf16[256,512]{1,0:T(8,128)(2,1)S(1)}, u32[]{:S(2)}, u32[]{:S(2)}) %collective-permute-start.4) | collective-permute-done | bytes 262176 | tf_op jit(solution)/shard_map/ppermute | solution.py:183
  33.3 1.8 %collective-permute-start.5 = (bf16[256,512]{1,0:T(8,128)(2,1)S(1)}, bf16[256,512]{1,0:T(8,128)(2,1)S(1)}, u32[]{:S(2)}, u32[]{:S(2)}) collective-permute-start(bf16[256,512]{1,0:T(8,128)(2,1)S(1)} %add_convert_fusion.5), channel_id=1, source_target_pairs={{2,4},{4,6},{6,7},{7,5},{5,3},{3,1},{1,0},{0,2},{10,12},{12,14},{1... | collective-permute-start | bytes 786440 | tf_op jit(solution)/shard_map/ppermute | solution.py:183
  36.2 3.8 %collective-permute-done.5 = bf16[256,512]{1,0:T(8,128)(2,1)S(1)} collective-permute-done((bf16[256,512]{1,0:T(8,128)(2,1)S(1)}, bf16[256,512]{1,0:T(8,128)(2,1)S(1)}, u32[]{:S(2)}, u32[]{:S(2)}) %collective-permute-start.5) | collective-permute-done | bytes 262176 | tf_op jit(solution)/shard_map/ppermute | solution.py:183
  40.1 1.8 %collective-permute-start.6 = (bf16[256,512]{1,0:T(8,128)(2,1)S(1)}, bf16[256,512]{1,0:T(8,128)(2,1)S(1)}, u32[]{:S(2)}, u32[]{:S(2)}) collective-permute-start(bf16[256,512]{1,0:T(8,128)(2,1)S(1)} %add_convert_fusion.4), channel_id=1, source_target_pairs={{2,4},{4,6},{6,7},{7,5},{5,3},{3,1},{1,0},{0,2},{10,12},{12,14},{1... | collective-permute-start | bytes 786440 | tf_op jit(solution)/shard_map/ppermute | solution.py:183
  42.9 3.6 %collective-permute-done.6 = bf16[256,512]{1,0:T(8,128)(2,1)S(1)} collective-permute-done((bf16[256,512]{1,0:T(8,128)(2,1)S(1)}, bf16[256,512]{1,0:T(8,128)(2,1)S(1)}, u32[]{:S(2)}, u32[]{:S(2)}) %collective-permute-start.6) | collective-permute-done | bytes 262176 | tf_op jit(solution)/shard_map/ppermute | solution.py:183
  46.5 1.9 %collective-permute-done.10 = bf16[256,512]{1,0:T(8,128)(2,1)S(1)} collective-permute-done((bf16[256,512]{1,0:T(8,128)(2,1)S(1)}, bf16[256,512]{1,0:T(8,128)(2,1)S(1)}, u32[]{:S(2)}, u32[]{:S(2)}) %collective-permute-start.10) | collective-permute-done | bytes 262176 | tf_op jit(solution)/shard_map/ppermute | solution.py:184
  48.6 1.6 %collective-permute-start.11 = (bf16[256,512]{1,0:T(8,128)(2,1)S(1)}, bf16[256,512]{1,0:T(8,128)(2,1)S(1)}, u32[]{:S(2)}, u32[]{:S(2)}) collective-permute-start(bf16[256,512]{1,0:T(8,128)(2,1)S(1)} %multiply_convert_fusion), channel_id=1, source_target_pairs={{2,4},{4,6},{6,7},{7,5},{5,3},{3,1},{1,0},{0,2},{10,12},{12,14},{1... | collective-permute-start | bytes 786440 | tf_op jit(solution)/shard_map/ppermute | solution.py:218
  51.5 5.7 %collective-permute-done.11 = bf16[256,512]{1,0:T(8,128)(2,1)S(1)} collective-permute-done((bf16[256,512]{1,0:T(8,128)(2,1)S(1)}, bf16[256,512]{1,0:T(8,128)(2,1)S(1)}, u32[]{:S(2)}, u32[]{:S(2)}) %collective-permute-start.11) | collective-permute-done | bytes 262176 | tf_op jit(solution)/shard_map/ppermute | solution.py:218
  57.2 1.6 %collective-permute-start.13 = (bf16[256,512]{1,0:T(8,128)(2,1)S(1)}, bf16[256,512]{1,0:T(8,128)(2,1)S(1)}, u32[]{:S(2)}, u32[]{:S(2)}) collective-permute-start(bf16[256,512]{1,0:T(8,128)(2,1)S(1)} %collective-permute-done.11), channel_id=1, source_target_pairs={{2,4},{4,6},{6,7},{7,5},{5,3},{3,1},{1,0},{0,2},{10,12},{12,14},{1... | collective-permute-start | bytes 786440 | tf_op jit(solution)/shard_map/ppermute | solution.py:218
  60.3 5.9 %collective-permute-done.13 = bf16[256,512]{1,0:T(8,128)(2,1)S(1)} collective-permute-done((bf16[256,512]{1,0:T(8,128)(2,1)S(1)}, bf16[256,512]{1,0:T(8,128)(2,1)S(1)}, u32[]{:S(2)}, u32[]{:S(2)}) %collective-permute-start.13) | collective-permute-done | bytes 262176 | tf_op jit(solution)/shard_map/ppermute | solution.py:218
  66.2 1.6 %collective-permute-start.15 = (bf16[256,512]{1,0:T(8,128)(2,1)S(1)}, bf16[256,512]{1,0:T(8,128)(2,1)S(1)}, u32[]{:S(2)}, u32[]{:S(2)}) collective-permute-start(bf16[256,512]{1,0:T(8,128)(2,1)S(1)} %collective-permute-done.13), channel_id=1, source_target_pairs={{2,4},{4,6},{6,7},{7,5},{5,3},{3,1},{1,0},{0,2},{10,12},{12,14},{1... | collective-permute-start | bytes 786440 | tf_op jit(solution)/shard_map/ppermute | solution.py:218
  69.0 4.0 %collective-permute-done.15 = bf16[256,512]{1,0:T(8,128)(2,1)S(1)} collective-permute-done((bf16[256,512]{1,0:T(8,128)(2,1)S(1)}, bf16[256,512]{1,0:T(8,128)(2,1)S(1)}, u32[]{:S(2)}, u32[]{:S(2)}) %collective-permute-start.15) | collective-permute-done | bytes 262176 | tf_op jit(solution)/shard_map/ppermute | solution.py:218
  73.0 1.6 %collective-permute-start.17 = (bf16[128,512]{1,0:T(8,128)(2,1)S(1)}, bf16[128,512]{1,0:T(8,128)(2,1)S(1)}, u32[]{:S(2)}, u32[]{:S(2)}) collective-permute-start(bf16[128,512]{1,0:T(8,128)(2,1)S(1)} %slice.18), channel_id=1, source_target_pairs={{2,4},{4,6},{6,7},{7,5},{5,3},{3,1},{1,0},{0,2},{10,12},{12,14},{1... | collective-permute-start | bytes 393224 | tf_op jit(solution)/shard_map/ppermute | solution.py:218
  74.7 0.7 collective-permute-start.18
  76.2 1.9 %collective-permute-done.17 = bf16[128,512]{1,0:T(8,128)(2,1)S(1)} collective-permute-done((bf16[128,512]{1,0:T(8,128)(2,1)S(1)}, bf16[128,512]{1,0:T(8,128)(2,1)S(1)}, u32[]{:S(2)}, u32[]{:S(2)}) %collective-permute-start.17) | collective-permute-done | bytes 131104 | tf_op jit(solution)/shard_map/ppermute | solution.py:218
  78.0 1.8 %collective-permute-done.18 = bf16[128,512]{1,0:T(8,128)(2,1)S(1)} collective-permute-done((bf16[128,512]{1,0:T(8,128)(2,1)S(1)}, bf16[128,512]{1,0:T(8,128)(2,1)S(1)}, u32[]{:S(2)}, u32[]{:S(2)}) %collective-permute-start.18) | collective-permute-done | bytes 131104 | tf_op jit(solution)/shard_map/ppermute | solution.py:219
  80.3 0.6 fusion.42
  81.0 0.6 fusion.45
  81.6 1.3 %collective-permute-done.19 = bf16[2,256,512]{2,1,0:T(8,128)(2,1)S(1)} collective-permute-done((bf16[2,256,512]{2,1,0:T(8,128)(2,1)S(1)}, bf16[2,256,512]{2,1,0:T(8,128)(2,1)S(1)}, u32[]{:S(2)}, u32[]{:S(2)}) %collective-permute-start.19) | collective-permute-done | bytes 524320 | tf_op jit(solution)/shard_map/ppermute | solution.py:252
  83.0 0.6 fusion.36
  83.9 1.5 %collective-permute-start.20 = (bf16[2,256,512]{2,1,0:T(8,128)(2,1)S(1)}, bf16[2,256,512]{2,1,0:T(8,128)(2,1)S(1)}, u32[]{:S(2)}, u32[]{:S(2)}) collective-permute-start(bf16[2,256,512]{2,1,0:T(8,128)(2,1)S(1)} %add_convert_fusion), channel_id=1, source_target_pairs={{0,16},{8,24},{16,0},{24,8},{1,17},{9,25},{17,1},{25,9},{2,18},{10... | collective-permute-start | bytes 1572872 | tf_op jit(solution)/shard_map/ppermute | solution.py:259
  85.4 0.6 fusion.39
  86.2 11.9 %collective-permute-done.20 = bf16[2,256,512]{2,1,0:T(8,128)(2,1)S(1)} collective-permute-done((bf16[2,256,512]{2,1,0:T(8,128)(2,1)S(1)}, bf16[2,256,512]{2,1,0:T(8,128)(2,1)S(1)}, u32[]{:S(2)}, u32[]{:S(2)}) %collective-permute-start.20) | collective-permute-done | bytes 524320 | tf_op jit(solution)/shard_map/ppermute | solution.py:259
  98.3 1.3 %copy.51 = f32[2,512,256]{2,1,0:T(8,128)} copy(f32[2,512,256]{1,2,0:T(8,128)S(1)} %add_bitcast_fusion) | data formatting | bytes 2097152 | tf_op jit(solution)/shard_map/transpose | solution.py:262
  (73 shorter events, 14.8 us)
Async XLA Ops:
  0.0 6.6 %collective-permute-start = (bf16[1024,256]{1,0:T(8,128)(2,1)}, bf16[1024,256]{1,0:T(8,128)(2,1)S(1)}, u32[]{:S(2)}, u32[]{:S(2)}) collective-permute-start(bf16[1024,256]{1,0:T(8,128)(2,1)} %param.8), channel_id=1, source_target_pairs={{0,8},{8,0},{16,24},{24,16},{1,9},{9,1},{17,25},{25,17},{2,10},{10... | collective-permute-start | bytes 1572872 | tf_op jit(solution)/shard_map/ppermute | solution.py:153
  0.5 15.3 %collective-permute-start.1 = (bf16[1024,256]{1,0:T(8,128)(2,1)}, bf16[1024,256]{1,0:T(8,128)(2,1)S(1)}, u32[]{:S(2)}, u32[]{:S(2)}) collective-permute-start(bf16[1024,256]{1,0:T(8,128)(2,1)} %param.8), channel_id=1, source_target_pairs={{0,16},{8,24},{16,0},{24,8},{1,17},{9,25},{17,1},{25,9},{2,18},{10... | collective-permute-start | bytes 1572872 | tf_op jit(solution)/shard_map/ppermute | solution.py:150
  3.9 11.9 %copy-start.1 = (bf16[8,8,96,512]{3,2,1,0:T(8,128)(2,1)S(1)}, bf16[8,8,96,512]{3,2,1,0:T(8,128)(2,1)}, u32[]{:S(2)}) copy-start(bf16[8,8,96,512]{3,2,1,0:T(8,128)(2,1)} %param.6) | copy-start | bytes 18874372
  16.4 3.2 %slice-start = ((s8[6291456]{0:T(1024)(128)(4,1)}), s8[4194304]{0:T(1024)(128)(4,1)S(1)}, s32[]{:S(2)}) async-start(s8[6291456]{0:T(1024)(128)(4,1)} %bitcast.239), calls=%async_computation | async-start | bytes 8388608
  17.0 2.0 %collective-permute-start.2 = (bf16[1024,256]{1,0:T(8,128)(2,1)S(1)}, bf16[1024,256]{1,0:T(8,128)(2,1)S(1)}, u32[]{:S(2)}, u32[]{:S(2)}) collective-permute-start(bf16[1024,256]{1,0:T(8,128)(2,1)S(1)} %collective-permute-done.1), channel_id=1, source_target_pairs={{0,8},{8,0},{16,24},{24,16},{1,9},{9,1},{17,25},{25,17},{2,10},{10... | collective-permute-start | bytes 1572872 | tf_op jit(solution)/shard_map/ppermute | solution.py:153
  17.1 2.5 %slice-start.1 = ((s8[6291456]{0:T(1024)(128)(4,1)}), s8[2097152]{0:T(1024)(128)(4,1)S(1)}, s32[]{:S(2)}) async-start(s8[6291456]{0:T(1024)(128)(4,1)} %bitcast.239), calls=%async_computation.1 | async-start | bytes 4194304
  20.1 5.6 %collective-permute-start.3 = (bf16[128,512]{1,0:T(8,128)(2,1)S(1)}, bf16[128,512]{1,0:T(8,128)(2,1)S(1)}, u32[]{:S(2)}, u32[]{:S(2)}) collective-permute-start(bf16[128,512]{1,0:T(8,128)(2,1)S(1)} %get-tuple-element.31), channel_id=1, source_target_pairs={{2,4},{4,6},{6,7},{7,5},{5,3},{3,1},{1,0},{0,2},{10,12},{12,14},{1... | collective-permute-start | bytes 393224 | tf_op jit(solution)/shard_map/ppermute | solution.py:183
  22.7 5.3 %collective-permute-start.7 = (bf16[128,512]{1,0:T(8,128)(2,1)S(1)}, bf16[128,512]{1,0:T(8,128)(2,1)S(1)}, u32[]{:S(2)}, u32[]{:S(2)}) collective-permute-start(bf16[128,512]{1,0:T(8,128)(2,1)S(1)} %get-tuple-element.32), channel_id=1, source_target_pairs={{4,2},{6,4},{7,6},{5,7},{3,5},{1,3},{0,1},{2,0},{12,10},{14,12},{1... | collective-permute-start | bytes 393224 | tf_op jit(solution)/shard_map/ppermute | solution.py:184
  25.7 7.5 %collective-permute-start.4 = (bf16[256,512]{1,0:T(8,128)(2,1)S(1)}, bf16[256,512]{1,0:T(8,128)(2,1)S(1)}, u32[]{:S(2)}, u32[]{:S(2)}) collective-permute-start(bf16[256,512]{1,0:T(8,128)(2,1)S(1)} %add_convert_fusion.6), channel_id=1, source_target_pairs={{2,4},{4,6},{6,7},{7,5},{5,3},{3,1},{1,0},{0,2},{10,12},{12,14},{1... | collective-permute-start | bytes 786440 | tf_op jit(solution)/shard_map/ppermute | solution.py:183
  28.1 14.3 %copy-start = (bf16[512,256]{1,0:T(8,128)(2,1)S(1)}, bf16[512,256]{1,0:T(8,128)(2,1)}, u32[]{:S(2)}) copy-start(bf16[512,256]{1,0:T(8,128)(2,1)} %source.1) | copy-start | bytes 786436
  28.1 7.3 %collective-permute-start.8 = (bf16[256,512]{1,0:T(8,128)(2,1)S(1)}, bf16[256,512]{1,0:T(8,128)(2,1)S(1)}, u32[]{:S(2)}, u32[]{:S(2)}) collective-permute-start(bf16[256,512]{1,0:T(8,128)(2,1)S(1)} %add_convert_fusion.3), channel_id=1, source_target_pairs={{4,2},{6,4},{7,6},{5,7},{3,5},{1,3},{0,1},{2,0},{12,10},{14,12},{1... | collective-permute-start | bytes 786440 | tf_op jit(solution)/shard_map/ppermute | solution.py:184
  33.3 6.7 %collective-permute-start.5 = (bf16[256,512]{1,0:T(8,128)(2,1)S(1)}, bf16[256,512]{1,0:T(8,128)(2,1)S(1)}, u32[]{:S(2)}, u32[]{:S(2)}) collective-permute-start(bf16[256,512]{1,0:T(8,128)(2,1)S(1)} %add_convert_fusion.5), channel_id=1, source_target_pairs={{2,4},{4,6},{6,7},{7,5},{5,3},{3,1},{1,0},{0,2},{10,12},{12,14},{1... | collective-permute-start | bytes 786440 | tf_op jit(solution)/shard_map/ppermute | solution.py:183
  35.4 6.5 %collective-permute-start.9 = (bf16[256,512]{1,0:T(8,128)(2,1)S(1)}, bf16[256,512]{1,0:T(8,128)(2,1)S(1)}, u32[]{:S(2)}, u32[]{:S(2)}) collective-permute-start(bf16[256,512]{1,0:T(8,128)(2,1)S(1)} %add_convert_fusion.2), channel_id=1, source_target_pairs={{4,2},{6,4},{7,6},{5,7},{3,5},{1,3},{0,1},{2,0},{12,10},{14,12},{1... | collective-permute-start | bytes 786440 | tf_op jit(solution)/shard_map/ppermute | solution.py:184
  40.1 6.4 %collective-permute-start.6 = (bf16[256,512]{1,0:T(8,128)(2,1)S(1)}, bf16[256,512]{1,0:T(8,128)(2,1)S(1)}, u32[]{:S(2)}, u32[]{:S(2)}) collective-permute-start(bf16[256,512]{1,0:T(8,128)(2,1)S(1)} %add_convert_fusion.4), channel_id=1, source_target_pairs={{2,4},{4,6},{6,7},{7,5},{5,3},{3,1},{1,0},{0,2},{10,12},{12,14},{1... | collective-permute-start | bytes 786440 | tf_op jit(solution)/shard_map/ppermute | solution.py:183
  42.0 6.4 %collective-permute-start.10 = (bf16[256,512]{1,0:T(8,128)(2,1)S(1)}, bf16[256,512]{1,0:T(8,128)(2,1)S(1)}, u32[]{:S(2)}, u32[]{:S(2)}) collective-permute-start(bf16[256,512]{1,0:T(8,128)(2,1)S(1)} %add_convert_fusion.1), channel_id=1, source_target_pairs={{4,2},{6,4},{7,6},{5,7},{3,5},{1,3},{0,1},{2,0},{12,10},{14,12},{1... | collective-permute-start | bytes 786440 | tf_op jit(solution)/shard_map/ppermute | solution.py:184
  48.6 8.5 %collective-permute-start.11 = (bf16[256,512]{1,0:T(8,128)(2,1)S(1)}, bf16[256,512]{1,0:T(8,128)(2,1)S(1)}, u32[]{:S(2)}, u32[]{:S(2)}) collective-permute-start(bf16[256,512]{1,0:T(8,128)(2,1)S(1)} %multiply_convert_fusion), channel_id=1, source_target_pairs={{2,4},{4,6},{6,7},{7,5},{5,3},{3,1},{1,0},{0,2},{10,12},{12,14},{1... | collective-permute-start | bytes 786440 | tf_op jit(solution)/shard_map/ppermute | solution.py:218
  50.3 8.8 %collective-permute-start.12 = (bf16[256,512]{1,0:T(8,128)(2,1)S(1)}, bf16[256,512]{1,0:T(8,128)(2,1)S(1)}, u32[]{:S(2)}, u32[]{:S(2)}) collective-permute-start(bf16[256,512]{1,0:T(8,128)(2,1)S(1)} %multiply_convert_fusion), channel_id=1, source_target_pairs={{4,2},{6,4},{7,6},{5,7},{3,5},{1,3},{0,1},{2,0},{12,10},{14,12},{1... | collective-permute-start | bytes 786440 | tf_op jit(solution)/shard_map/ppermute | solution.py:219
  57.2 9.0 %collective-permute-start.13 = (bf16[256,512]{1,0:T(8,128)(2,1)S(1)}, bf16[256,512]{1,0:T(8,128)(2,1)S(1)}, u32[]{:S(2)}, u32[]{:S(2)}) collective-permute-start(bf16[256,512]{1,0:T(8,128)(2,1)S(1)} %collective-permute-done.11), channel_id=1, source_target_pairs={{2,4},{4,6},{6,7},{7,5},{5,3},{3,1},{1,0},{0,2},{10,12},{12,14},{1... | collective-permute-start | bytes 786440 | tf_op jit(solution)/shard_map/ppermute | solution.py:218
  59.0 8.7 %collective-permute-start.14 = (bf16[256,512]{1,0:T(8,128)(2,1)S(1)}, bf16[256,512]{1,0:T(8,128)(2,1)S(1)}, u32[]{:S(2)}, u32[]{:S(2)}) collective-permute-start(bf16[256,512]{1,0:T(8,128)(2,1)S(1)} %collective-permute-done.12), channel_id=1, source_target_pairs={{4,2},{6,4},{7,6},{5,7},{3,5},{1,3},{0,1},{2,0},{12,10},{14,12},{1... | collective-permute-start | bytes 786440 | tf_op jit(solution)/shard_map/ppermute | solution.py:219
  66.2 6.8 %collective-permute-start.15 = (bf16[256,512]{1,0:T(8,128)(2,1)S(1)}, bf16[256,512]{1,0:T(8,128)(2,1)S(1)}, u32[]{:S(2)}, u32[]{:S(2)}) collective-permute-start(bf16[256,512]{1,0:T(8,128)(2,1)S(1)} %collective-permute-done.13), channel_id=1, source_target_pairs={{2,4},{4,6},{6,7},{7,5},{5,3},{3,1},{1,0},{0,2},{10,12},{12,14},{1... | collective-permute-start | bytes 786440 | tf_op jit(solution)/shard_map/ppermute | solution.py:218
  67.8 6.9 %collective-permute-start.16 = (bf16[256,512]{1,0:T(8,128)(2,1)S(1)}, bf16[256,512]{1,0:T(8,128)(2,1)S(1)}, u32[]{:S(2)}, u32[]{:S(2)}) collective-permute-start(bf16[256,512]{1,0:T(8,128)(2,1)S(1)} %collective-permute-done.14), channel_id=1, source_target_pairs={{4,2},{6,4},{7,6},{5,7},{3,5},{1,3},{0,1},{2,0},{12,10},{14,12},{1... | collective-permute-start | bytes 786440 | tf_op jit(solution)/shard_map/ppermute | solution.py:219
  73.0 5.0 %collective-permute-start.17 = (bf16[128,512]{1,0:T(8,128)(2,1)S(1)}, bf16[128,512]{1,0:T(8,128)(2,1)S(1)}, u32[]{:S(2)}, u32[]{:S(2)}) collective-permute-start(bf16[128,512]{1,0:T(8,128)(2,1)S(1)} %slice.18), channel_id=1, source_target_pairs={{2,4},{4,6},{6,7},{7,5},{5,3},{3,1},{1,0},{0,2},{10,12},{12,14},{1... | collective-permute-start | bytes 393224 | tf_op jit(solution)/shard_map/ppermute | solution.py:218
  74.7 5.2 %collective-permute-start.18 = (bf16[128,512]{1,0:T(8,128)(2,1)S(1)}, bf16[128,512]{1,0:T(8,128)(2,1)S(1)}, u32[]{:S(2)}, u32[]{:S(2)}) collective-permute-start(bf16[128,512]{1,0:T(8,128)(2,1)S(1)} %slice.19), channel_id=1, source_target_pairs={{4,2},{6,4},{7,6},{5,7},{3,5},{1,3},{0,1},{2,0},{12,10},{14,12},{1... | collective-permute-start | bytes 393224 | tf_op jit(solution)/shard_map/ppermute | solution.py:219
  80.9 2.0 %collective-permute-start.19 = (bf16[2,256,512]{2,1,0:T(8,128)(2,1)S(1)}, bf16[2,256,512]{2,1,0:T(8,128)(2,1)S(1)}, u32[]{:S(2)}, u32[]{:S(2)}) collective-permute-start(bf16[2,256,512]{2,1,0:T(8,128)(2,1)S(1)} %fusion.42), channel_id=1, source_target_pairs={{0,8},{8,0},{16,24},{24,16},{1,9},{9,1},{17,25},{25,17},{2,10},{10... | collective-permute-start | bytes 1572872 | tf_op jit(solution)/shard_map/ppermute | solution.py:252
  83.7 2.3 %collective-permute-start.21 = (bf16[2,256,512]{2,1,0:T(8,128)(2,1)S(1)}, bf16[2,256,512]{2,1,0:T(8,128)(2,1)S(1)}, u32[]{:S(2)}, u32[]{:S(2)}) collective-permute-start(bf16[2,256,512]{2,1,0:T(8,128)(2,1)S(1)} %fusion.36), channel_id=1, source_target_pairs={{0,8},{8,0},{16,24},{24,16},{1,9},{9,1},{17,25},{25,17},{2,10},{10... | collective-permute-start | bytes 1572872 | tf_op jit(solution)/shard_map/ppermute | solution.py:252
  83.9 14.2 %collective-permute-start.20 = (bf16[2,256,512]{2,1,0:T(8,128)(2,1)S(1)}, bf16[2,256,512]{2,1,0:T(8,128)(2,1)S(1)}, u32[]{:S(2)}, u32[]{:S(2)}) collective-permute-start(bf16[2,256,512]{2,1,0:T(8,128)(2,1)S(1)} %add_convert_fusion), channel_id=1, source_target_pairs={{0,16},{8,24},{16,0},{24,8},{1,17},{9,25},{17,1},{25,9},{2,18},{10... | collective-permute-start | bytes 1572872 | tf_op jit(solution)/shard_map/ppermute | solution.py:259
